TPU v7x, 128 devices: a whole 4x4x4 slice. The times are simulated.
128 devices in a mesh: gx: 4 (over x), gy: 8 (over z, y_lo), gz: 4 (over y_hi, core).
Axes of the slice: x: 4, y: 4 (y_hi: 2, y_lo: 2; y = y_hi * 2 + y_lo), z: 4, core: 2. Of those that a mesh axis runs over, the one named last changes fastest.
Arguments:
- tokens: bfloat16 [4096, 6144], P('gy', ('gz', 'gx')), may hold values from -6 to 6
- weight: bfloat16 [6144, 24576], P('gz', ('gx', 'gy')), may hold values from -0.15625 to 0.15625
- bias: float32 [24576], P(('gx', 'gz')), may hold values from -4 to 4
Outputs:
- hidden: bfloat16 [4096, 24576], P('gy', ('gx', 'gz'))
All inputs are finite; a program needn't handle non-finite values.
Results may differ from a plain program's by a relative error of at most 0.001.
Values may be sent and summed in bfloat16 or wider, within the bound.
A program may use at most 128 MiB of HBM per device.

v0:
```python
import jax
import jax.numpy as jnp
from jax import lax
from jax.sharding import Mesh
from jax.sharding import PartitionSpec as P

GY = ("gy_0", "gy_1")
GX_GY = ("gx", "gy_0", "gy_1")


def in_order(blocks, dim):
    shape = list(blocks.shape[1:])
    shape[dim] *= blocks.shape[0]
    return jnp.moveaxis(blocks, 0, dim).reshape(shape)


def from_everyone(shard, axis):
    copies = jnp.broadcast_to(shard, (lax.axis_size(axis), *shard.shape))
    return lax.all_to_all(copies, axis, split_axis=0, concat_axis=0, tiled=True)


def gather_directly(shard, axis, dim):
    return in_order(from_everyone(shard, axis), dim)


def gather_axes(shard, axes, dim):
    if not axes:
        return shard
    nearer = lax.all_gather(shard, axes[-1], axis=dim, tiled=True)
    return gather_axes(nearer, axes[:-1], dim)


def per_device(tokens, weight, bias):
    features = gather_directly(tokens, "gx", 1)
    columns = gather_axes(weight, GY, 1)
    partial_sum = jnp.dot(features, columns, preferred_element_type=jnp.float32)
    owned = lax.psum_scatter(partial_sum, "gz", scatter_dimension=1, tiled=True)
    pre = owned + bias[None, :]
    return jax.nn.gelu(pre, approximate=False).astype(jnp.bfloat16)


def solution(mesh):
    torus = Mesh(
        mesh.devices.reshape(mesh.shape["gx"], 4, 2, mesh.shape["gz"]), ("gx", "gy_0", "gy_1", "gz")
    )
    placed = (P(GY, ("gz", "gx")), P("gz", GX_GY), P(("gx", "gz")))
    return jax.shard_map(
        per_device, mesh=torus, in_specs=placed, out_specs=P(GY, ("gx", "gz")), check_vma=False
    )
```

profile of v0, /device:TPU:1, one launch (start us, length us, event | category | flops | bytes accessed | tf_op | source)
XLA Modules:
  0.0 388.7 jit_solution(11253117486997832891)
XLA Ops:
  6.5 0.0 copy-start
  6.5 0.0 all-gather.3.cloned.1.call-start
  6.5 0.7 all-gather.3.cloned.1.call-update
  7.3 0.0 all-gather.5.cloned.1.call-start
  7.3 69.9 %all-gather.3.cloned.1.call-done = bf16[1536,1536]{1,0:T(8,128)(2,1)} async-done(((bf16[1536,768]{1,0:T(8,128)(2,1)}), bf16[1536,1536]{1,0:T(8,128)(2,1)}) %all-gather.3.cloned.1.call-update) | async-done | bytes 4718608 | tf_op jit(solution)/shard_map/all_gather | solution.py:29
  77.2 0.0 all-gather.5.cloned.1.call-update
  77.2 0.0 reduce-scatter.2.cloned.1.call-start
  77.3 0.0 copy-done
  77.3 0.2 copy.4
  77.5 0.1 broadcast_in_dim.4
  77.6 23.5 %all_to_all.5 = bf16[4,512,384]{1,2,0:T(8,128)(2,1)S(1)} all-to-all(bf16[4,512,384]{1,2,0:T(8,128)(2,1)S(1)} %broadcast_in_dim.4), channel_id=1, replica_groups=mesh['gx'=4,'gy_0'=4,'gy_1'=2,'gz'=4] {'gx'}, dimensions={0} | all-to-all | bytes 3145728 | tf_op jit(solution)/shard_map/all_to_all | solution.py:19
  101.1 151.4 %all-gather.5.cloned.1.call-done = bf16[1536,6144]{1,0:T(8,128)(2,1)} async-done(((bf16[1536,1536]{1,0:T(8,128)(2,1)}), bf16[1536,6144]{1,0:T(8,128)(2,1)}) %all-gather.5.cloned.1.call-update) | async-done | bytes 18874384 | tf_op jit(solution)/shard_map/all_gather | solution.py:29
  252.5 16.7 %fusion.10 = f32[512,6144]{1,0:T(8,128)} fusion(bf16[512,1536]{0,1:T(8,128)(2,1)S(1)} %bitcast.5, bf16[1536,6144]{1,0:T(8,128)(2,1)} %all-gather.5.cloned.1.call-done), kind=kOutput, calls=%fused_computation.19 | convolution fusion | flops 9663676416 | bytes 33030144 | tf_op jit(solution)/shard_map/dot_general | solution.py:36
  269.2 0.0 copy-start.1
  269.2 0.0 reduce-scatter.2.cloned.1.call-update
  269.2 104.1 %reduce-scatter.2.cloned.1.call-done = f32[512,1536]{1,0:T(8,128)} async-done(((f32[512,6144]{1,0:T(8,128)}), f32[512,1536]{1,0:T(8,128)}) %reduce-scatter.2.cloned.1.call-update) | async-done | bytes 3145744 | tf_op jit(solution)/shard_map/reduce_scatter | solution.py:37
  373.3 0.0 copy-done.1
  373.3 8.8 %fusion.2 = bf16[512,1536]{1,0:T(8,128)(2,1)} fusion(f32[512,1536]{1,0:T(8,128)} %reduce-scatter.2.cloned.1.call-done, f32[1536]{0:T(1024)S(1)} %copy-done.1), kind=kLoop, calls=%fused_computation.3 | loop fusion | flops 51904512 | bytes 4724736 | tf_op jit(solution)/shard_map/convert_element_type | solution.py:39
Async XLA Ops:
  6.5 70.7 %copy-start = (bf16[512,384]{1,0:T(8,128)(2,1)S(1)}, bf16[512,384]{1,0:T(8,128)(2,1)}, u32[]{:S(2)}) copy-start(bf16[512,384]{1,0:T(8,128)(2,1)} %param.3) | copy-start | bytes 1179652
  6.5 70.7 %all-gather.3.cloned.1.call-start = ((), (), s32[]{:S(2)}) async-start(), calls=%async_computation.2 | async-start | bytes 7077888 | tf_op jit(solution)/shard_map/all_gather | solution.py:29
  7.3 245.2 %all-gather.5.cloned.1.call-start = ((), (), s32[]{:S(2)}) async-start(), calls=%async_computation.3 | async-start | bytes 23592960 | tf_op jit(solution)/shard_map/all_gather | solution.py:29
  77.2 296.1 %reduce-scatter.2.cloned.1.call-start = ((), (), s32[]{:S(2)}) async-start(), calls=%async_computation.4 | async-start | bytes 15728640 | tf_op jit(solution)/shard_map/reduce_scatter | solution.py:37
  269.2 104.1 %copy-start.1 = (f32[1536]{0:T(1024)S(1)}, f32[1536]{0:T(1024)}, u32[]{:S(2)}) copy-start(f32[1536]{0:T(1024)} %param.5) | copy-start | bytes 18436
Sparse Core Ops, SparseCore 0:
  9.0 68.1 all-gather.2
  78.9 173.5 all-gather.4
  269.3 103.9 reduce-scatter.1
where the time goes:
time: 389 us
  waiting for transfers between devices  326 us (84%)
  blocking collectives  23.5 us (6%)
  matrix products  16.7 us (4%)
  between operations  13.1 us (3%)
  other arithmetic  8.84 us (2%)
    all_gather x2, waiting for transfers between devices, gather_axes(): nearer = lax.all_gather(shard, axes[-1], axis=dim, tiled=True)  221 us
    reduce_scatter x1, waiting for transfers between devices, per_device(): owned = lax.psum_scatter(partial_sum, 'gz', scatter_dimension=1, tiled=True)  104 us
    all_to_all x1, blocking collectives, from_everyone(): return lax.all_to_all(copies, axis, split_axis=0, concat_axis=0, tiled=True)  23.5 us
    dot_general x1, matrix products, per_device(): partial_sum = jnp.dot(features, columns, preferred_element_type=jnp.float32)  16.7 us
    convert_element_type x1, other arithmetic, per_device(): return jax.nn.gelu(pre, approximate=False).astype(jnp.bfloat16)  8.84 us
  transfers between devices with their start and end apart: 3, of which 3 were waited for; matrix products, arithmetic and copies ran while one was open for 0% of the time, Pallas kernels for 0%

commit v1 on v0

v1 whole, which is shorter than its diff:
```python
import jax
import jax.numpy as jnp
from jax import lax
from jax.experimental import pallas as pl
from jax.experimental.pallas import tpu as pltpu
from jax.sharding import Mesh
from jax.sharding import PartitionSpec as P

MESH = pl.DeviceIdType.MESH
S = 384
ROWS = 512
D = 6144
TILE = 256


def kernel(
    t_ref, w_ref, b_ref, o_ref,
    T, W, B, O,
    tsem, wsem, bsem, osem,
    ts_y, ts_x, ts_r, ws_a, ws_b, ws_n, ws_r, ws_f, bs, os,
):
    x, z, l, h, c = (lax.axis_index(a) for a in ("x", "z", "l", "h", "c"))
    y = 2 * h + l
    g = 2 * h + c
    other = 1 - c
    xp, xm, xf = (x + 1) % 4, (x + 3) % 4, (x + 2) % 4
    zp, zm, zf = (z + 1) % 4, (z + 3) % 4, (z + 2) % 4
    yp, ym = (y + 1) % 4, (y + 3) % 4
    order = [2 * hh + cc for hh in (h, 1 - h) for cc in (0, 1)]
    kinds = [g, 2 * (1 - h) + c]
    sibling = {"c": other}
    sends = []

    def token(gg, xx):
        return T.at[:, pl.ds(pl.multiple_of((gg * 4 + xx) * S, S), S)]

    def weight(zz, gg, i):
        return W.at[zz, pl.ds(pl.multiple_of(gg * 4 * S + i * S, S), S), :]

    def shard(i, half):
        return w_ref.at[pl.ds(i * S, S), pl.ds(pl.multiple_of(half * S, S), S)]

    def push(src, dst, send, recv, to):
        copy = pltpu.make_async_remote_copy(
            src_ref=src, dst_ref=dst, send_sem=send, recv_sem=recv,
            device_id=to, device_id_type=MESH,
        )
        copy.start()
        sends.append(copy)

    def landed(slot, sem):
        pltpu.make_async_copy(slot, slot, sem).wait()

    def push_token(gg, xx, send, to):
        push(token(gg, xx), token(gg, xx), send, tsem.at[gg, xx], to)

    def push_weight(zz, gg, i, send, to):
        push(weight(zz, gg, i), weight(zz, gg, i), send, wsem.at[zz, gg, i], to)

    @pl.when(c == l)
    def _():
        pltpu.make_async_copy(t_ref, token(g, x), tsem.at[g, x]).start()

    for i in range(4):
        pltpu.make_async_copy(shard(i, h), weight(z, g, i), wsem.at[z, g, i]).start()
    pltpu.make_async_copy(b_ref, B.at[0], bsem.at[0]).start()

    barrier = pltpu.get_barrier_semaphore()
    peers = [
        {"l": (l + dl) % 2, "h": (h + dh) % 2, "c": (c + dc) % 2}
        for dl in (0, 1) for dh in (0, 1) for dc in (0, 1) if dl + dh + dc
    ]
    peers += [{"x": xp}, {"x": xm}, {"z": zp}, {"z": zm}]
    for peer in peers:
        pl.semaphore_signal(barrier, inc=1, device_id=peer, device_id_type=MESH)
    pl.semaphore_wait(barrier, len(peers))

    def to_own_chip():
        return pltpu.make_async_remote_copy(
            src_ref=t_ref, dst_ref=token(g, x), send_sem=ts_y.at[3], recv_sem=tsem.at[g, x],
            device_id=sibling, device_id_type=MESH,
        )

    @pl.when(c != l)
    def _():
        to_own_chip().start()

    for k, yy in enumerate((yp, ym, (y + 2) % 4)):
        push(t_ref, token(g, x), ts_y.at[k], tsem.at[g, x], {"l": yy % 2, "h": yy // 2, "c": l})
    for i in range(4):
        push(shard(i, h), weight(z, g, i), ws_a.at[i, 0], wsem.at[z, g, i], {"z": zp})
        push(shard(i, h), weight(z, g, i), ws_a.at[i, 1], wsem.at[z, g, i], {"z": zm})
        push(shard(i, 1 - h), weight(z, g, i), ws_a.at[i, 3], wsem.at[z, g, i], {"h": 1 - h})
        push(shard(i, h), weight(z, g, i), ws_a.at[i, 2], wsem.at[z, g, i], sibling)
    for k, (dh, dc) in enumerate(((0, 1), (1, 0), (1, 1))):
        to = {"h": (h + dh) % 2, "c": (c + dc) % 2}
        push(b_ref, B.at[1 + k], bs.at[k], bsem.at[1 + k], to)

    def token_y(q):
        gg = order[q]
        landed(token(gg, x), tsem.at[gg, x])
        push_token(gg, x, ts_x.at[q, 0], {"x": xp})
        push_token(gg, x, ts_x.at[q, 1], {"x": xm})

    def token_x(q):
        gg = order[q]
        landed(token(gg, xm), tsem.at[gg, xm])
        if q % 2 == 0:
            push_token(gg, xm, ts_r.at[q], {"x": xp})
        landed(token(gg, xp), tsem.at[gg, xp])
        if q % 2 == 1:
            push_token(gg, xp, ts_r.at[q], {"x": xm})

    def token_far(q):
        gg = order[q]
        landed(token(gg, xf), tsem.at[gg, xf])

    def weight_y(i):
        gg = kinds[1]
        landed(weight(z, gg, i), wsem.at[z, gg, i])
        push_weight(z, gg, i, ws_b.at[i, 0], {"z": zp})
        push_weight(z, gg, i, ws_b.at[i, 1], {"z": zm})
        push_weight(z, gg, i, ws_b.at[i, 2], sibling)

    def weight_z(kind, i):
        gg = kinds[kind]
        landed(weight(zm, gg, i), wsem.at[zm, gg, i])
        if i % 2 == 0:
            push_weight(zm, gg, i, ws_r.at[kind, i], {"z": zp})
        push_weight(zm, gg, i, ws_n.at[0, kind, i], sibling)
        landed(weight(zp, gg, i), wsem.at[zp, gg, i])
        if i % 2 == 1:
            push_weight(zp, gg, i, ws_r.at[kind, i], {"z": zm})
        push_weight(zp, gg, i, ws_n.at[1, kind, i], sibling)

    def weight_far(kind, i):
        gg = kinds[kind]
        landed(weight(zf, gg, i), wsem.at[zf, gg, i])
        push_weight(zf, gg, i, ws_f.at[kind, i], sibling)

    def from_sibling(zz):
        for hh in (0, 1):
            for i in range(4):
                gg = 2 * hh + other
                landed(weight(zz, gg, i), wsem.at[zz, gg, i])

    def out_slot(ll, hh):
        return o_ref.at[:, pl.ds(pl.multiple_of((2 * ll + hh) * S, S), S)]

    def out_remote(zz, k):
        return pltpu.make_async_remote_copy(
            src_ref=O.at[k], dst_ref=out_slot(l, h), send_sem=os.at[k], recv_sem=osem.at[2 * l + h],
            device_id={"l": c, "h": zz // 2, "c": zz % 2}, device_id_type=MESH,
        )

    def out_local(k):
        return pltpu.make_async_copy(O.at[k], out_slot(l, h), osem.at[2 * l + h])

    def mine(zz):
        return jnp.logical_and(c == l, zz == g)

    def columns(zz, k):
        which = 2 * ((zz // 2 + h) % 2) + (zz % 2 + c) % 2
        bias = B[which, :, pl.ds(pl.multiple_of((2 * l + h) * S, S), S)]

        @pl.loop(0, ROWS // TILE)
        def _(m):
            rows = pl.ds(pl.multiple_of(m * TILE, TILE), TILE)
            pre = jnp.dot(T[rows, :], W[zz], preferred_element_type=jnp.float32) + bias
            act = pre * (1.0 + lax.erf(pre * 0.7071067811865476)) * 0.5
            O[k, rows, :] = act.astype(jnp.bfloat16)

        @pl.when(mine(zz))
        def _():
            out_local(k).start()

        @pl.when(jnp.logical_not(mine(zz)))
        def _():
            out_remote(zz, k).start()

    token_y(0)
    token_y(1)
    weight_z(0, 0)
    token_y(2)
    token_y(3)
    weight_z(0, 1)
    weight_y(0)
    token_x(0)
    weight_z(0, 2)
    token_x(1)
    weight_y(1)
    weight_z(0, 3)
    token_x(2)
    weight_y(2)
    weight_z(1, 0)
    token_x(3)
    weight_y(3)
    weight_z(1, 1)
    weight_z(1, 2)
    for i in range(4):
        landed(weight(z, g, i), wsem.at[z, g, i])
    landed(B.at[0], bsem.at[0])
    for k in range(3):
        landed(B.at[1 + k], bsem.at[1 + k])
    for q in range(4):
        token_far(q)
    from_sibling(z)
    columns(z, 0)
    weight_z(1, 3)
    from_sibling(zm)
    columns(zm, 1)
    for i in range(4):
        weight_far(0, i)
    from_sibling(zp)
    columns(zp, 2)
    for i in range(4):
        weight_far(1, i)
    from_sibling(zf)
    columns(zf, 3)

    for ll in (0, 1):
        for hh in (0, 1):
            landed(out_slot(ll, hh), osem.at[2 * ll + hh])

    for copy in sends:
        copy.wait_send()

    @pl.when(c != l)
    def _():
        to_own_chip().wait_send()

    for k, zz in enumerate((z, zm, zp, zf)):
        @pl.when(jnp.logical_not(mine(zz)))
        def _():
            out_remote(zz, k).wait_send()


def per_device(tokens, weight, bias):
    any_spec = pl.BlockSpec(memory_space=pl.ANY)
    dma = pltpu.SemaphoreType.DMA
    return pl.pallas_call(
        kernel,
        out_shape=jax.ShapeDtypeStruct((ROWS, 4 * S), jnp.bfloat16),
        in_specs=[any_spec] * 3,
        out_specs=any_spec,
        scratch_shapes=[
            pltpu.VMEM((ROWS, D), jnp.bfloat16),
            pltpu.VMEM((4, D, S), jnp.bfloat16),
            pltpu.VMEM((4, 1, 4 * S), jnp.float32),
            pltpu.VMEM((4, ROWS, S), jnp.bfloat16),
            dma((4, 4)), dma((4, 4, 4)), dma((4,)), dma((4,)),
            dma((4,)), dma((4, 2)), dma((4,)), dma((4, 4)), dma((4, 3)),
            dma((2, 2, 4)), dma((2, 4)), dma((2, 4)), dma((3,)), dma((4,)),
        ],
        compiler_params=pltpu.CompilerParams(
            collective_id=0, has_side_effects=True, vmem_limit_bytes=60 * 2**20
        ),
    )(tokens, weight, bias.reshape(1, 4 * S))


def solution(mesh):
    torus = Mesh(mesh.devices.reshape(4, 4, 2, 2, 2), ("x", "z", "l", "h", "c"))
    placed = (P(("z", "l"), ("h", "c", "x")), P(("h", "c"), ("x", "z", "l")), P(("x", "h", "c")))
    return jax.shard_map(
        per_device, mesh=torus, in_specs=placed, out_specs=P(("z", "l"), ("x", "h", "c")), check_vma=False
    )
```

time: 389 us -> 109 us (0.28)
  waiting for transfers between devices: 326 us -> 0 us
  Pallas kernels: 0 us -> 104 us
  blocking collectives: 23.5 us -> 0 us
  matrix products: 16.7 us -> 0 us
  between operations: 13.1 us -> 0.01 us
  other arithmetic: 8.84 us -> 0 us
    all_gather x2 -> x0, waiting for transfers between devices: 221 us -> none  [gather_axes(): nearer = lax.all_gather(shard, axes[-1], axis=dim, tiled=True)]
    pallas_call x0 -> x1, Pallas kernels: none -> 104 us  [per_device(): pl.pallas_call(kernel, out_shape=jax.ShapeDtypeStruct((ROWS, 4 * S), jnp....]
    reduce_scatter x1 -> x0, waiting for transfers between devices: 104 us -> none  [per_device(): owned = lax.psum_scatter(partial_sum, 'gz', scatter_dimension=1, tiled=True)]
    all_to_all x1 -> x0, blocking collectives: 23.5 us -> none  [from_everyone(): return lax.all_to_all(copies, axis, split_axis=0, concat_axis=0, tiled=True)]
    dot_general x1 -> x0, matrix products: 16.7 us -> none  [per_device(): partial_sum = jnp.dot(features, columns, preferred_element_type=jnp.float32)]
    convert_element_type x1 -> x0, other arithmetic: 8.84 us -> none  [per_device(): return jax.nn.gelu(pre, approximate=False).astype(jnp.bfloat16)]
  transfers between devices with their start and end apart: 3 -> 0, of which waited for: 3 -> 0; matrix products, arithmetic and copies ran while one was open for 0% -> 0% of each run, Pallas kernels for 0% -> 0%
where the time goes in v1:
time: 109 us; the launch traced here: 108 us
  Pallas kernels  104 us (95%)
  local copies, waits for them, and re-layouts  3.95 us (4%)
    pallas_call x1, Pallas kernels, per_device(): pl.pallas_call(kernel, out_shape=jax.ShapeDtypeStruct((ROWS, 4 * S), jnp....  104 us
    unnamed x1, local copies, waits for them, and re-layouts  2.65 us

profile of v1, /device:TPU:1, one launch (start us, length us, event | category | flops | bytes accessed | tf_op | source)
XLA Modules:
  0.0 108.4 jit_solution(17190028556220955106)
XLA Ops:
  0.0 1.3 %reshape.3.b_ref = f32[1,1536]{1,0:T(1,128)} reshape(f32[1536]{0:T(1024)} %param.5) | data formatting | bytes 12288 | tf_op jit(solution)/shard_map/reshape | solution.py:258
  1.3 104.5 %shard_map.37 = bf16[512,1536]{1,0:T(8,128)(2,1)} custom-call(bf16[512,384]{1,0:T(8,128)(2,1)} %t_ref.1, bf16[1536,768]{1,0:T(8,128)(2,1)} %w_ref.1, f32[1,1536]{1,0:T(1,128)} %reshape.3.b_ref), custom_call_target="tpu_custom_call" | custom-call | tf_op jit(solution)/shard_map/pallas_call | solution.py:241
  105.8 2.7 %copy.5 = bf16[512,1536]{1,0:T(8,128)(2,1)} copy(bf16[512,1536]{1,0:T(8,128)(2,1)} %shard_map.37) | data formatting | bytes 3145728

commit v2 on v1

--- a/solution.py
+++ b/solution.py
@@ -11,6 +11,8 @@
 ROWS = 512
 D = 6144
 TILE = 256
+C = 128
+QUARTER = 1536
 
 
 def kernel(
@@ -35,10 +37,10 @@
         return T.at[:, pl.ds(pl.multiple_of((gg * 4 + xx) * S, S), S)]
 
     def weight(zz, gg, i):
-        return W.at[zz, pl.ds(pl.multiple_of(gg * 4 * S + i * S, S), S), :]
+        return W.at[zz, pl.ds(pl.multiple_of(gg * QUARTER, QUARTER), QUARTER), pl.ds(i * C, C)]
 
     def shard(i, half):
-        return w_ref.at[pl.ds(i * S, S), pl.ds(pl.multiple_of(half * S, S), S)]
+        return w_ref.at[:, pl.ds(pl.multiple_of(half * S + i * C, C), C)]
 
     def push(src, dst, send, recv, to):
         copy = pltpu.make_async_remote_copy(
@@ -61,7 +63,7 @@
     def _():
         pltpu.make_async_copy(t_ref, token(g, x), tsem.at[g, x]).start()
 
-    for i in range(4):
+    for i in range(3):
         pltpu.make_async_copy(shard(i, h), weight(z, g, i), wsem.at[z, g, i]).start()
     pltpu.make_async_copy(b_ref, B.at[0], bsem.at[0]).start()
 
@@ -87,7 +89,7 @@
 
     for k, yy in enumerate((yp, ym, (y + 2) % 4)):
         push(t_ref, token(g, x), ts_y.at[k], tsem.at[g, x], {"l": yy % 2, "h": yy // 2, "c": l})
-    for i in range(4):
+    for i in range(3):
         push(shard(i, h), weight(z, g, i), ws_a.at[i, 0], wsem.at[z, g, i], {"z": zp})
         push(shard(i, h), weight(z, g, i), ws_a.at[i, 1], wsem.at[z, g, i], {"z": zm})
         push(shard(i, 1 - h), weight(z, g, i), ws_a.at[i, 3], wsem.at[z, g, i], {"h": 1 - h})
@@ -125,98 +127,114 @@
     def weight_z(kind, i):
         gg = kinds[kind]
         landed(weight(zm, gg, i), wsem.at[zm, gg, i])
-        if i % 2 == 0:
-            push_weight(zm, gg, i, ws_r.at[kind, i], {"z": zp})
         push_weight(zm, gg, i, ws_n.at[0, kind, i], sibling)
         landed(weight(zp, gg, i), wsem.at[zp, gg, i])
-        if i % 2 == 1:
-            push_weight(zp, gg, i, ws_r.at[kind, i], {"z": zm})
         push_weight(zp, gg, i, ws_n.at[1, kind, i], sibling)
+
+    def relay(kind, i):
+        if kind == 0:
+            push_weight(zm, kinds[0], i, ws_r.at[0, i], {"z": zp})
+        else:
+            push_weight(zp, kinds[1], i, ws_r.at[1, i], {"z": zm})
 
     def weight_far(kind, i):
         gg = kinds[kind]
         landed(weight(zf, gg, i), wsem.at[zf, gg, i])
         push_weight(zf, gg, i, ws_f.at[kind, i], sibling)
 
-    def from_sibling(zz):
+    def from_sibling(zz, i):
         for hh in (0, 1):
-            for i in range(4):
-                gg = 2 * hh + other
-                landed(weight(zz, gg, i), wsem.at[zz, gg, i])
-
-    def out_slot(ll, hh):
-        return o_ref.at[:, pl.ds(pl.multiple_of((2 * ll + hh) * S, S), S)]
-
-    def out_remote(zz, k):
+            gg = 2 * hh + other
+            landed(weight(zz, gg, i), wsem.at[zz, gg, i])
+
+    def out_slot(ll, hh, first=0, width=S):
+        return o_ref.at[:, pl.ds(pl.multiple_of((2 * ll + hh) * S + first, C), width)]
+
+    def out_remote(zz, k, first, width):
         return pltpu.make_async_remote_copy(
-            src_ref=O.at[k], dst_ref=out_slot(l, h), send_sem=os.at[k], recv_sem=osem.at[2 * l + h],
+            src_ref=O.at[k, :, pl.ds(first, width)], dst_ref=out_slot(l, h, first, width),
+            send_sem=os.at[k, first // C], recv_sem=osem.at[2 * l + h],
             device_id={"l": c, "h": zz // 2, "c": zz % 2}, device_id_type=MESH,
         )
 
-    def out_local(k):
-        return pltpu.make_async_copy(O.at[k], out_slot(l, h), osem.at[2 * l + h])
+    def out_local(k, first, width):
+        return pltpu.make_async_copy(
+            O.at[k, :, pl.ds(first, width)], out_slot(l, h, first, width), osem.at[2 * l + h]
+        )
 
     def mine(zz):
         return jnp.logical_and(c == l, zz == g)
 
-    def columns(zz, k):
+    def columns(zz, k, first=0, width=S):
         which = 2 * ((zz // 2 + h) % 2) + (zz % 2 + c) % 2
-        bias = B[which, :, pl.ds(pl.multiple_of((2 * l + h) * S, S), S)]
+        parts = [
+            B[which, pl.ds((2 * l + h) * 3 + t, 1), :] for t in range(first // C, (first + width) // C)
+        ]
+        bias = jnp.concatenate(parts, axis=1) if len(parts) > 1 else parts[0]
 
         @pl.loop(0, ROWS // TILE)
         def _(m):
             rows = pl.ds(pl.multiple_of(m * TILE, TILE), TILE)
-            pre = jnp.dot(T[rows, :], W[zz], preferred_element_type=jnp.float32) + bias
+            pre = jnp.dot(
+                T[rows, :], W[zz, :, pl.ds(first, width)], preferred_element_type=jnp.float32
+            ) + bias
             act = pre * (1.0 + lax.erf(pre * 0.7071067811865476)) * 0.5
-            O[k, rows, :] = act.astype(jnp.bfloat16)
+            O[k, rows, pl.ds(first, width)] = act.astype(jnp.bfloat16)
 
         @pl.when(mine(zz))
         def _():
-            out_local(k).start()
+            out_local(k, first, width).start()
 
         @pl.when(jnp.logical_not(mine(zz)))
         def _():
-            out_remote(zz, k).start()
+            out_remote(zz, k, first, width).start()
 
     token_y(0)
     token_y(1)
     weight_z(0, 0)
+    weight_y(0)
     token_y(2)
     token_y(3)
     weight_z(0, 1)
-    weight_y(0)
+    weight_y(1)
     token_x(0)
     weight_z(0, 2)
     token_x(1)
-    weight_y(1)
-    weight_z(0, 3)
+    weight_y(2)
+    for i in range(3):
+        relay(0, i)
+    weight_z(1, 0)
+    relay(1, 0)
     token_x(2)
-    weight_y(2)
-    weight_z(1, 0)
+    weight_z(1, 1)
+    relay(1, 1)
     token_x(3)
-    weight_y(3)
-    weight_z(1, 1)
     weight_z(1, 2)
-    for i in range(4):
+    relay(1, 2)
+    for i in range(3):
         landed(weight(z, g, i), wsem.at[z, g, i])
     landed(B.at[0], bsem.at[0])
     for k in range(3):
         landed(B.at[1 + k], bsem.at[1 + k])
     for q in range(4):
         token_far(q)
-    from_sibling(z)
+    for i in range(3):
+        from_sibling(z, i)
     columns(z, 0)
-    weight_z(1, 3)
-    from_sibling(zm)
+    for i in range(3):
+        from_sibling(zm, i)
     columns(zm, 1)
-    for i in range(4):
-        weight_far(0, i)
-    from_sibling(zp)
+    weight_far(0, 0)
+    weight_far(1, 0)
+    for i in range(3):
+        from_sibling(zp, i)
     columns(zp, 2)
-    for i in range(4):
-        weight_far(1, i)
-    from_sibling(zf)
-    columns(zf, 3)
+    for i in range(3):
+        if i:
+            weight_far(0, i)
+            weight_far(1, i)
+        from_sibling(zf, i)
+        columns(zf, 3, i * C, C)
 
     for ll in (0, 1):
         for hh in (0, 1):
@@ -229,10 +247,11 @@
     def _():
         to_own_chip().wait_send()
 
-    for k, zz in enumerate((z, zm, zp, zf)):
+    whole = [(zz, k, 0, S) for k, zz in enumerate((z, zm, zp))]
+    for zz, *where in whole + [(zf, 3, i * C, C) for i in range(3)]:
         @pl.when(jnp.logical_not(mine(zz)))
         def _():
-            out_remote(zz, k).wait_send()
+            out_remote(zz, *where).wait_send()
 
 
 def per_device(tokens, weight, bias):
@@ -241,21 +260,21 @@
     return pl.pallas_call(
         kernel,
         out_shape=jax.ShapeDtypeStruct((ROWS, 4 * S), jnp.bfloat16),
-        in_specs=[any_spec] * 3,
+        in_specs=[pl.BlockSpec(memory_space=pltpu.HBM)] * 3,
         out_specs=any_spec,
         scratch_shapes=[
             pltpu.VMEM((ROWS, D), jnp.bfloat16),
             pltpu.VMEM((4, D, S), jnp.bfloat16),
-            pltpu.VMEM((4, 1, 4 * S), jnp.float32),
+            pltpu.VMEM((4, 12, C), jnp.float32),
             pltpu.VMEM((4, ROWS, S), jnp.bfloat16),
-            dma((4, 4)), dma((4, 4, 4)), dma((4,)), dma((4,)),
-            dma((4,)), dma((4, 2)), dma((4,)), dma((4, 4)), dma((4, 3)),
-            dma((2, 2, 4)), dma((2, 4)), dma((2, 4)), dma((3,)), dma((4,)),
+            dma((4, 4)), dma((4, 4, 3)), dma((4,)), dma((4,)),
+            dma((4,)), dma((4, 2)), dma((4,)), dma((3, 4)), dma((3, 3)),
+            dma((2, 2, 3)), dma((2, 3)), dma((2, 3)), dma((3,)), dma((4, 3)),
         ],
         compiler_params=pltpu.CompilerParams(
-            collective_id=0, has_side_effects=True, vmem_limit_bytes=60 * 2**20
+            collective_id=0, has_side_effects=True, vmem_limit_bytes=48 * 2**20
         ),
-    )(tokens, weight, bias.reshape(1, 4 * S))
+    )(*(pltpu.with_memory_space_constraint(a, pltpu.HBM) for a in (tokens, weight, bias.reshape(12, C))))
 
 
 def solution(mesh):

time: 109 us -> 102 us (0.936)
  the two profiles are of different devices: /device:TPU:1 before, /device:TPU:97 now
where the time goes in v2:
time: 102 us
  Pallas kernels  101 us (99%)
  local copies, waits for them, and re-layouts  1.15 us (1%)
    pallas_call x1, Pallas kernels, per_device(): pl.pallas_call(kernel, out_shape=jax.ShapeDtypeStruct((ROWS, 4 * S), jnp....  101 us

profile of v2, /device:TPU:97, one launch (start us, length us, event | category | flops | bytes accessed | tf_op | source)
XLA Modules:
  0.0 101.9 jit_solution(2617594086158168263)
XLA Ops:
  0.0 100.8 %shard_map.37 = bf16[512,1536]{1,0:T(8,128)(2,1)S(1)} custom-call(bf16[512,384]{1,0:T(8,128)(2,1)} %t_ref.1, bf16[1536,768]{1,0:T(8,128)(2,1)} %w_ref.1, f32[12,128]{1,0:T(8,128)} %bitcast.1), custom_call_target="tpu_custom_call" | custom-call | tf_op jit(solution)/shard_map/pallas_call | solution.py:260
  100.8 1.1 %copy.5 = bf16[512,1536]{1,0:T(8,128)(2,1)} copy(bf16[512,1536]{1,0:T(8,128)(2,1)S(1)} %shard_map.37) | data formatting | bytes 3145728

commit v3 on v2

v3 whole, which is shorter than its diff:
```python
import jax
import jax.numpy as jnp
from jax import lax
from jax.experimental import pallas as pl
from jax.experimental.pallas import tpu as pltpu
from jax.sharding import Mesh
from jax.sharding import PartitionSpec as P

MESH = pl.DeviceIdType.MESH
S = 384
C = 128
ROWS = 512
D = 6144
TILE = 256

PAIR = 2 * S
HALF = 4 * PAIR


def kernel(
    t_ref, w_ref, b_ref, o_ref,
    T, W, G, B, A, O,
    lsem, tsem, wsem, bsem, osem,
    ts_y, ts_x, ts_r, ws_a, ws_b, ws_n, ws_r, ws_f, bs, os,
):
    x, z, l, h, c = (lax.axis_index(a) for a in ("x", "z", "l", "h", "c"))
    y = 2 * h + l
    g = 2 * h + c
    other = 1 - c
    xp, xm = (x + 1) % 4, (x + 3) % 4
    zp, zm, zf = (z + 1) % 4, (z + 3) % 4, (z + 2) % 4
    yp, ym = (y + 1) % 4, (y + 3) % 4
    sibling = {"c": other}
    sends = []

    def half_rows(part):
        return pl.ds(part * TILE, TILE)

    def token(hk, r, cc, part):
        return T.at[half_rows(part), pl.ds(pl.multiple_of(hk * HALF + r * PAIR + cc * S, S), S)]

    def weight(zz, hk, cc, i):
        if zz is zf and i >= 2:
            return W.at[zz, hk, pl.ds(2 * (i - 2), 2), cc, :, pl.ds(2 * C, C)]
        return W.at[zz, hk, :, cc, :, pl.ds(i * C, C)]

    def push(src, dst, send, recv, to):
        copy = pltpu.make_async_remote_copy(
            src_ref=src, dst_ref=dst, send_sem=send, recv_sem=recv,
            device_id=to, device_id_type=MESH,
        )
        copy.start()
        sends.append(copy)

    def landed(slot, sem):
        pltpu.make_async_copy(slot, slot, sem).wait()

    def push_token(q, r, r_there, part, send, to):
        hk, cc = divmod(q, 2)
        push(token(hk, r, cc, part), token(hk, r_there, cc, part), send, tsem.at[hk, r_there, cc, part], to)

    def push_weight(zz, kind, i, send, to):
        push(weight(zz, kind, c, i), weight(zz, kind, c, i), send, wsem.at[zz, kind, c, i], to)

    @pl.when(c == l)
    def _():
        for part in (0, 1):
            pltpu.make_async_copy(t_ref.at[half_rows(part)], token(0, 1, c, part), tsem.at[0, 1, c, part]).start()

    def stage(half, slot, row, k):
        src = w_ref.at[pl.ds(row * S, S), pl.ds(pl.multiple_of(half * S, S), S)]
        return pltpu.make_async_copy(src, slot, lsem.at[k, row])

    staged = [
        [stage(h, W.at[z, 0, (row - x + 5) % 4, c], row, 0) for row in range(4)],
        [stage(1 - h, G.at[(row - x + 5) % 4], row, 1) for row in range(4)],
    ]
    for copies in staged:
        for copy in copies:
            copy.start()
    pltpu.make_async_copy(b_ref, B.at[0], bsem.at[0]).start()

    barrier = pltpu.get_barrier_semaphore()
    peers = [
        {"l": (l + dl) % 2, "h": (h + dh) % 2, "c": (c + dc) % 2}
        for dl in (0, 1) for dh in (0, 1) for dc in (0, 1) if dl + dh + dc
    ]
    peers += [{"x": xp}, {"x": xm}, {"z": zp}, {"z": zm}]
    for peer in peers:
        pl.semaphore_signal(barrier, inc=1, device_id=peer, device_id_type=MESH)
    for copy in staged[0]:
        copy.wait()
    pl.semaphore_wait(barrier, len(peers))

    def to_own_chip(part):
        return pltpu.make_async_remote_copy(
            src_ref=t_ref.at[half_rows(part)], dst_ref=token(0, 1, c, part),
            send_sem=ts_y.at[3, part], recv_sem=tsem.at[0, 1, c, part],
            device_id=sibling, device_id_type=MESH,
        )

    @pl.when(c != l)
    def _():
        to_own_chip(0).start()
        to_own_chip(1).start()

    def token_column(part):
        for k, yy in enumerate((yp, ym, (y + 2) % 4)):
            hk = (yy // 2 + h) % 2
            push(
                t_ref.at[half_rows(part)], token(hk, 1, c, part), ts_y.at[k, part], tsem.at[hk, 1, c, part],
                {"l": yy % 2, "h": yy // 2, "c": l},
            )

    def weight_column(i):
        push(G.at[:, :, pl.ds(i * C, C)], weight(z, 1, c, i), ws_a.at[i, 3], wsem.at[z, 1, c, i], {"h": 1 - h})

    for i in range(3):
        push_weight(z, 0, i, ws_a.at[i, 0], {"z": zp})
        push_weight(z, 0, i, ws_a.at[i, 1], {"z": zm})
    token_column(0)
    for copy in staged[1]:
        copy.wait()
    weight_column(0)
    token_column(1)
    weight_column(1)
    weight_column(2)
    for i in range(3):
        push_weight(z, 0, i, ws_a.at[i, 2], sibling)
    for k, (dh, dc) in enumerate(((0, 1), (1, 0), (1, 1))):
        to = {"h": (h + dh) % 2, "c": (c + dc) % 2}
        push(b_ref, B.at[1 + k], bs.at[k], bsem.at[1 + k], to)

    def token_in(q, r, part):
        hk, cc = divmod(q, 2)
        landed(token(hk, r, cc, part), tsem.at[hk, r, cc, part])

    def token_y(q, part):
        token_in(q, 1, part)
        push_token(q, 1, 0, part, ts_x.at[q, 0, part], {"x": xp})
        push_token(q, 1, 2, part, ts_x.at[q, 1, part], {"x": xm})

    def token_x(q, part):
        token_in(q, 0, part)
        if q % 2 == 0:
            push_token(q, 0, 3, part, ts_r.at[q, part], {"x": xp})
        token_in(q, 2, part)
        if q % 2 == 1:
            push_token(q, 2, 3, part, ts_r.at[q, part], {"x": xm})

    def weight_in(zz, kind, cc, i):
        landed(weight(zz, kind, cc, i), wsem.at[zz, kind, cc, i])

    def weight_y(i):
        weight_in(z, 1, c, i)
        push_weight(z, 1, i, ws_b.at[i, 0], {"z": zp})
        push_weight(z, 1, i, ws_b.at[i, 1], {"z": zm})
        push_weight(z, 1, i, ws_b.at[i, 2], sibling)

    def weight_z(kind, i):
        weight_in(zm, kind, c, i)
        push_weight(zm, kind, i, ws_n.at[0, kind, i], sibling)
        weight_in(zp, kind, c, i)
        push_weight(zp, kind, i, ws_n.at[1, kind, i], sibling)

    def relay(kind, i):
        near, to = ((zm, zp), (zp, zm))[kind]

        def part(r, count):
            return W.at[near, kind, pl.ds(r, count), c, :, pl.ds(i * C, C)]

        for k, slot in enumerate([part(0, 4)] if i < 2 else [part(0, 2), part(2, 2)]):
            push(slot, slot, ws_r.at[kind, i + k], wsem.at[near, kind, c, i + k], {"z": to})

    def weight_far(kind, i):
        weight_in(zf, kind, c, i)
        push_weight(zf, kind, i, ws_f.at[kind, i], sibling)

    def from_sibling(zz):
        for kind in (0, 1):
            for i in range(3):
                weight_in(zz, kind, other, i)

    def out_slot(ll, hh, rows=pl.ds(0, ROWS), first=0, width=S):
        return o_ref.at[rows, pl.ds(pl.multiple_of((2 * ll + hh) * S + first, C), width)]

    def out_remote(zz, k, rows, first, width):
        return pltpu.make_async_remote_copy(
            src_ref=O.at[k, rows, pl.ds(first, width)], dst_ref=out_slot(l, h, rows, first, width),
            send_sem=os.at[k, first // C], recv_sem=osem.at[2 * l + h],
            device_id={"l": c, "h": zz // 2, "c": zz % 2}, device_id_type=MESH,
        )

    def out_local(k, rows, first, width):
        return pltpu.make_async_copy(
            O.at[k, rows, pl.ds(first, width)], out_slot(l, h, rows, first, width), osem.at[2 * l + h]
        )

    def mine(zz):
        return jnp.logical_and(c == l, zz == g)

    def dot(rows, start, count, w):
        return jnp.dot(
            T[rows, pl.ds(start, count)], w.reshape(count, w.shape[-1]), preferred_element_type=jnp.float32
        )

    def finish(zz, k, part, first, width, product):
        which = 2 * ((zz // 2 + h) % 2) + (zz % 2 + c) % 2
        parts = [
            B[which, pl.ds((2 * l + h) * 3 + t, 1), :] for t in range(first // C, (first + width) // C)
        ]
        bias = jnp.concatenate(parts, axis=1) if len(parts) > 1 else parts[0]
        rows = half_rows(part)
        pre = product + bias
        act = pre * (1.0 + lax.erf(pre * 0.7071067811865476)) * 0.5
        O[k, rows, pl.ds(first, width)] = act.astype(jnp.bfloat16)

        @pl.when(mine(zz))
        def _():
            out_local(k, rows, first, width).start()

        @pl.when(jnp.logical_not(mine(zz)))
        def _():
            out_remote(zz, k, rows, first, width).start()

    def columns(zz, k, part):
        finish(zz, k, part, 0, S, dot(half_rows(part), 0, D, W[zz]))

    def far_columns(i, part):
        finish(zf, 3, part, i * C, C, dot(half_rows(part), 0, D, W[zf, :, :, :, :, pl.ds(i * C, C)]))

    def last_columns(half, part):
        rows = half_rows(part)
        w = [W[zf, kind, pl.ds(2 * half, 2), :, :, pl.ds(2 * C, C)] for kind in (0, 1)]
        product = sum(dot(rows, kind * HALF + half * 2 * PAIR, 2 * PAIR, w[kind]) for kind in (0, 1))
        if half == 0:
            A[rows, :] = product
        else:
            finish(zf, 3, part, 2 * C, C, product + A[rows, :])

    for q in range(4):
        token_y(q, 0)
    weight_z(0, 0)
    token_x(0, 0)
    token_x(1, 0)
    token_y(0, 1)
    token_y(1, 1)
    token_x(2, 0)
    weight_z(0, 1)
    weight_y(0)
    token_x(3, 0)
    token_y(2, 1)
    token_y(3, 1)
    weight_z(0, 2)
    weight_y(1)
    token_x(0, 1)
    token_x(1, 1)
    weight_y(2)
    for i in range(3):
        relay(0, i)
    weight_z(1, 0)
    relay(1, 0)
    token_x(2, 1)
    weight_z(1, 1)
    relay(1, 1)
    token_x(3, 1)
    for k in range(4):
        landed(B.at[k], bsem.at[k])
    for q in range(4):
        token_in(q, 3, 0)
    from_sibling(z)
    columns(z, 0, 0)
    weight_z(1, 2)
    relay(1, 2)
    from_sibling(zm)
    columns(zm, 1, 0)
    from_sibling(zp)
    columns(zp, 2, 0)
    for q in range(4):
        token_in(q, 3, 1)
    columns(z, 0, 1)
    columns(zm, 1, 1)
    columns(zp, 2, 1)
    for i in range(4):
        for kind in (0, 1):
            weight_far(kind, i)
        for kind in (0, 1):
            weight_in(zf, kind, other, i)
        for part in (0, 1):
            if i < 2:
                far_columns(i, part)
            else:
                last_columns(i - 2, part)

    for ll in (0, 1):
        for hh in (0, 1):
            landed(out_slot(ll, hh), osem.at[2 * ll + hh])

    for copy in sends:
        copy.wait_send()

    @pl.when(c != l)
    def _():
        to_own_chip(0).wait_send()
        to_own_chip(1).wait_send()

    all_rows = pl.ds(0, ROWS)
    whole = [(zz, k, all_rows, 0, S) for k, zz in enumerate((z, zm, zp))]
    for zz, *where in whole + [(zf, 3, all_rows, i * C, C) for i in range(3)]:
        @pl.when(jnp.logical_not(mine(zz)))
        def _():
            out_remote(zz, *where).wait_send()


def per_device(tokens, weight, bias):
    any_spec = pl.BlockSpec(memory_space=pl.ANY)
    dma = pltpu.SemaphoreType.DMA
    in_hbm = [pltpu.with_memory_space_constraint(a, pltpu.HBM) for a in (tokens, weight, bias.reshape(12, C))]
    return pl.pallas_call(
        kernel,
        out_shape=jax.ShapeDtypeStruct((ROWS, 4 * S), jnp.bfloat16),
        in_specs=[pl.BlockSpec(memory_space=pltpu.HBM)] * 3,
        out_specs=any_spec,
        scratch_shapes=[
            pltpu.VMEM((ROWS, D), jnp.bfloat16),
            pltpu.VMEM((4, 2, 4, 2, S, S), jnp.bfloat16),
            pltpu.VMEM((4, S, S), jnp.bfloat16),
            pltpu.VMEM((4, 12, C), jnp.float32),
            pltpu.VMEM((ROWS, C), jnp.float32),
            pltpu.VMEM((4, ROWS, S), jnp.bfloat16),
            dma((2, 4)), dma((2, 4, 2, 2)), dma((4, 2, 2, 4)), dma((4,)), dma((4,)),
            dma((4, 2)), dma((4, 2, 2)), dma((4, 2)), dma((3, 4)), dma((3, 3)),
            dma((2, 2, 3)), dma((2, 4)), dma((2, 4)), dma((3,)), dma((4, 3)),
        ],
        compiler_params=pltpu.CompilerParams(
            collective_id=0, has_side_effects=True, vmem_limit_bytes=48 * 2**20
        ),
    )(*in_hbm)


def solution(mesh):
    torus = Mesh(mesh.devices.reshape(4, 4, 2, 2, 2), ("x", "z", "l", "h", "c"))
    placed = (P(("z", "l"), ("h", "c", "x")), P(("h", "c"), ("x", "z", "l")), P(("x", "h", "c")))
    return jax.shard_map(
        per_device, mesh=torus, in_specs=placed, out_specs=P(("z", "l"), ("x", "h", "c")), check_vma=False
    )
```

time: 102 us -> 96.1 us (0.942)
  the two profiles are of different devices: /device:TPU:97 before, /device:TPU:1 now
where the time goes in v3:
time: 96.1 us; the launch traced here: 96 us
  Pallas kernels  94.8 us (99%)
  local copies, waits for them, and re-layouts  1.15 us (1%)
    pallas_call x1, Pallas kernels, per_device(): pl.pallas_call(kernel, out_shape=jax.ShapeDtypeStruct((ROWS, 4 * S), jnp....  94.8 us

profile of v3, /device:TPU:1, one launch (start us, length us, event | category | flops | bytes accessed | tf_op | source)
XLA Modules:
  0.0 96.0 jit_solution(9275219347939812823)
XLA Ops:
  0.0 94.8 %shard_map.37 = bf16[512,1536]{1,0:T(8,128)(2,1)S(1)} custom-call(bf16[512,384]{1,0:T(8,128)(2,1)} %t_ref.1, bf16[1536,768]{1,0:T(8,128)(2,1)} %w_ref.1, f32[12,128]{1,0:T(8,128)} %bitcast.1), custom_call_target="tpu_custom_call" | custom-call | tf_op jit(solution)/shard_map/pallas_call | solution.py:319
  94.9 1.1 %copy.5 = bf16[512,1536]{1,0:T(8,128)(2,1)} copy(bf16[512,1536]{1,0:T(8,128)(2,1)S(1)} %shard_map.37) | data formatting | bytes 3145728

commit v4 on v3

--- a/solution.py
+++ b/solution.py
@@ -104,8 +104,9 @@
         to_own_chip(0).start()
         to_own_chip(1).start()
 
-    def token_column(part):
-        for k, yy in enumerate((yp, ym, (y + 2) % 4)):
+    def token_column(part, steps=(0, 1, 2)):
+        for k in steps:
+            yy = (yp, ym, (y + 2) % 4)[k]
             hk = (yy // 2 + h) % 2
             push(
                 t_ref.at[half_rows(part)], token(hk, 1, c, part), ts_y.at[k, part], tsem.at[hk, 1, c, part],
@@ -122,9 +123,10 @@
     for copy in staged[1]:
         copy.wait()
     weight_column(0)
-    token_column(1)
+    token_column(1, (0, 1))
     weight_column(1)
     weight_column(2)
+    token_column(1, (2,))
     for i in range(3):
         push_weight(z, 0, i, ws_a.at[i, 2], sibling)
     for k, (dh, dc) in enumerate(((0, 1), (1, 0), (1, 1))):
@@ -243,26 +245,26 @@
     weight_z(0, 0)
     token_x(0, 0)
     token_x(1, 0)
+    weight_y(0)
+    weight_z(0, 1)
+    token_x(2, 0)
+    token_x(3, 0)
     token_y(0, 1)
     token_y(1, 1)
-    token_x(2, 0)
-    weight_z(0, 1)
-    weight_y(0)
-    token_x(3, 0)
-    token_y(2, 1)
-    token_y(3, 1)
     weight_z(0, 2)
     weight_y(1)
+    weight_z(1, 0)
     token_x(0, 1)
-    token_x(1, 1)
     weight_y(2)
     for i in range(3):
         relay(0, i)
-    weight_z(1, 0)
     relay(1, 0)
-    token_x(2, 1)
+    token_x(1, 1)
+    token_y(2, 1)
+    token_y(3, 1)
     weight_z(1, 1)
     relay(1, 1)
+    token_x(2, 1)
     token_x(3, 1)
     for k in range(4):
         landed(B.at[k], bsem.at[k])

time: 96.1 us -> 94.7 us (0.985)
  Pallas kernels: 94.8 us -> 93.2 us
    pallas_call x1, Pallas kernels: 94.8 us -> 93.2 us  [per_device(): pl.pallas_call(kernel, out_shape=jax.ShapeDtypeStruct((ROWS, 4 * S), jnp....]
where the time goes in v4:
time: 94.7 us; the launch traced here: 94.4 us
  Pallas kernels  93.2 us (98%)
  local copies, waits for them, and re-layouts  1.15 us (1%)
    pallas_call x1, Pallas kernels, per_device(): pl.pallas_call(kernel, out_shape=jax.ShapeDtypeStruct((ROWS, 4 * S), jnp....  93.2 us

profile of v4, /device:TPU:1, one launch (start us, length us, event | category | flops | bytes accessed | tf_op | source)
XLA Modules:
  0.0 94.4 jit_solution(6849503406433978727)
XLA Ops:
  0.0 93.2 %shard_map.37 = bf16[512,1536]{1,0:T(8,128)(2,1)S(1)} custom-call(bf16[512,384]{1,0:T(8,128)(2,1)} %t_ref.1, bf16[1536,768]{1,0:T(8,128)(2,1)} %w_ref.1, f32[12,128]{1,0:T(8,128)} %bitcast.1), custom_call_target="tpu_custom_call" | custom-call | tf_op jit(solution)/shard_map/pallas_call | solution.py:321
  93.2 1.1 %copy.5 = bf16[512,1536]{1,0:T(8,128)(2,1)} copy(bf16[512,1536]{1,0:T(8,128)(2,1)S(1)} %shard_map.37) | data formatting | bytes 3145728

commit v5 on v4

--- a/solution.py
+++ b/solution.py
@@ -62,6 +62,14 @@
     def push_weight(zz, kind, i, send, to):
         push(weight(zz, kind, c, i), weight(zz, kind, c, i), send, wsem.at[zz, kind, c, i], to)
 
+    barrier = pltpu.get_barrier_semaphore()
+    peers = [{"z": zp}, {"z": zm}, {"x": xp}, {"x": xm}]
+    peers += [
+        {"l": (l + dl) % 2, "h": (h + dh) % 2, "c": (c + dc) % 2}
+        for dl in (0, 1) for dh in (0, 1) for dc in (0, 1) if dl + dh + dc
+    ]
+    for peer in peers:
+        pl.semaphore_signal(barrier, inc=1, device_id=peer, device_id_type=MESH)
     @pl.when(c == l)
     def _():
         for part in (0, 1):
@@ -80,14 +88,6 @@
             copy.start()
     pltpu.make_async_copy(b_ref, B.at[0], bsem.at[0]).start()
 
-    barrier = pltpu.get_barrier_semaphore()
-    peers = [
-        {"l": (l + dl) % 2, "h": (h + dh) % 2, "c": (c + dc) % 2}
-        for dl in (0, 1) for dh in (0, 1) for dc in (0, 1) if dl + dh + dc
-    ]
-    peers += [{"x": xp}, {"x": xm}, {"z": zp}, {"z": zm}]
-    for peer in peers:
-        pl.semaphore_signal(barrier, inc=1, device_id=peer, device_id_type=MESH)
     for copy in staged[0]:
         copy.wait()
     pl.semaphore_wait(barrier, len(peers))
@@ -206,13 +206,12 @@
             T[rows, pl.ds(start, count)], w.reshape(count, w.shape[-1]), preferred_element_type=jnp.float32
         )
 
-    def finish(zz, k, part, first, width, product):
+    def finish(zz, k, rows, first, width, product):
         which = 2 * ((zz // 2 + h) % 2) + (zz % 2 + c) % 2
         parts = [
             B[which, pl.ds((2 * l + h) * 3 + t, 1), :] for t in range(first // C, (first + width) // C)
         ]
         bias = jnp.concatenate(parts, axis=1) if len(parts) > 1 else parts[0]
-        rows = half_rows(part)
         pre = product + bias
         act = pre * (1.0 + lax.erf(pre * 0.7071067811865476)) * 0.5
         O[k, rows, pl.ds(first, width)] = act.astype(jnp.bfloat16)
@@ -226,19 +225,18 @@
             out_remote(zz, k, rows, first, width).start()
 
     def columns(zz, k, part):
-        finish(zz, k, part, 0, S, dot(half_rows(part), 0, D, W[zz]))
+        finish(zz, k, half_rows(part), 0, S, dot(half_rows(part), 0, D, W[zz]))
 
     def far_columns(i, part):
-        finish(zf, 3, part, i * C, C, dot(half_rows(part), 0, D, W[zf, :, :, :, :, pl.ds(i * C, C)]))
-
-    def last_columns(half, part):
-        rows = half_rows(part)
+        finish(zf, 3, half_rows(part), i * C, C, dot(half_rows(part), 0, D, W[zf, :, :, :, :, pl.ds(i * C, C)]))
+
+    def last_columns(half, rows):
         w = [W[zf, kind, pl.ds(2 * half, 2), :, :, pl.ds(2 * C, C)] for kind in (0, 1)]
         product = sum(dot(rows, kind * HALF + half * 2 * PAIR, 2 * PAIR, w[kind]) for kind in (0, 1))
         if half == 0:
             A[rows, :] = product
         else:
-            finish(zf, 3, part, 2 * C, C, product + A[rows, :])
+            finish(zf, 3, rows, 2 * C, C, product + A[rows, :])
 
     for q in range(4):
         token_y(q, 0)
@@ -288,15 +286,15 @@
             weight_far(kind, i)
         for kind in (0, 1):
             weight_in(zf, kind, other, i)
-        for part in (0, 1):
-            if i < 2:
-                far_columns(i, part)
-            else:
-                last_columns(i - 2, part)
-
-    for ll in (0, 1):
-        for hh in (0, 1):
-            landed(out_slot(ll, hh), osem.at[2 * ll + hh])
+        if i < 2:
+            far_columns(i, 0)
+            far_columns(i, 1)
+        elif i == 2:
+            for part in (0, 1):
+                last_columns(0, half_rows(part))
+        else:
+            for first in range(0, ROWS, 128):
+                last_columns(1, pl.ds(first, 128))
 
     for copy in sends:
         copy.wait_send()
@@ -305,6 +303,11 @@
     def _():
         to_own_chip(0).wait_send()
         to_own_chip(1).wait_send()
+
+    for ll in (0, 1):
+        for hh in (0, 1):
+            landed(out_slot(ll, hh), osem.at[2 * ll + hh])
+
 
     all_rows = pl.ds(0, ROWS)
     whole = [(zz, k, all_rows, 0, S) for k, zz in enumerate((z, zm, zp))]

time: 94.7 us -> 94.4 us (level)
  no operation moved by 1% of the time
where the time goes in v5:
time: 94.4 us; the launch traced here: 94.3 us
  Pallas kernels  93.1 us (99%)
  local copies, waits for them, and re-layouts  1.15 us (1%)
    pallas_call x1, Pallas kernels, per_device(): pl.pallas_call(kernel, out_shape=jax.ShapeDtypeStruct((ROWS, 4 * S), jnp....  93.1 us

profile of v5, /device:TPU:1, one launch (start us, length us, event | category | flops | bytes accessed | tf_op | source)
XLA Modules:
  0.0 94.3 jit_solution(11570664486764204196)
XLA Ops:
  0.0 93.1 %shard_map.37 = bf16[512,1536]{1,0:T(8,128)(2,1)S(1)} custom-call(bf16[512,384]{1,0:T(8,128)(2,1)} %t_ref.1, bf16[1536,768]{1,0:T(8,128)(2,1)} %w_ref.1, f32[12,128]{1,0:T(8,128)} %bitcast.1), custom_call_target="tpu_custom_call" | custom-call | tf_op jit(solution)/shard_map/pallas_call | solution.py:324
  93.1 1.1 %copy.5 = bf16[512,1536]{1,0:T(8,128)(2,1)} copy(bf16[512,1536]{1,0:T(8,128)(2,1)S(1)} %shard_map.37) | data formatting | bytes 3145728

commit v6 on v5

--- a/solution.py
+++ b/solution.py
@@ -174,9 +174,26 @@
         for k, slot in enumerate([part(0, 4)] if i < 2 else [part(0, 2), part(2, 2)]):
             push(slot, slot, ws_r.at[kind, i + k], wsem.at[near, kind, c, i + k], {"z": to})
 
-    def weight_far(kind, i):
-        weight_in(zf, kind, c, i)
-        push_weight(zf, kind, i, ws_f.at[kind, i], sibling)
+    def far_to_sibling(kind, i):
+        slot = weight(zf, kind, c, i)
+        return pltpu.make_async_remote_copy(
+            src_ref=slot, dst_ref=slot, send_sem=ws_f.at[kind, i], recv_sem=wsem.at[zf, kind, c, i],
+            device_id=sibling, device_id_type=MESH,
+        )
+
+    def weight_far(i):
+        def in_turn(kinds):
+            for kind in kinds:
+                weight_in(zf, kind, c, i)
+                far_to_sibling(kind, i).start()
+
+        @pl.when(z == 0)
+        def _():
+            in_turn((1, 0))
+
+        @pl.when(z != 0)
+        def _():
+            in_turn((0, 1))
 
     def from_sibling(zz):
         for kind in (0, 1):
@@ -282,8 +299,7 @@
     columns(zm, 1, 1)
     columns(zp, 2, 1)
     for i in range(4):
-        for kind in (0, 1):
-            weight_far(kind, i)
+        weight_far(i)
         for kind in (0, 1):
             weight_in(zf, kind, other, i)
         if i < 2:
@@ -298,6 +314,9 @@
 
     for copy in sends:
         copy.wait_send()
+    for i in range(4):
+        for kind in (0, 1):
+            far_to_sibling(kind, i).wait_send()
 
     @pl.when(c != l)
     def _():

time: 94.4 us -> 94.4 us (level)
  no operation moved by 1% of the time
where the time goes in v6:
time: 94.4 us; the launch traced here: 94.3 us
  Pallas kernels  93.1 us (99%)
  local copies, waits for them, and re-layouts  1.15 us (1%)
    pallas_call x1, Pallas kernels, per_device(): pl.pallas_call(kernel, out_shape=jax.ShapeDtypeStruct((ROWS, 4 * S), jnp....  93.1 us

profile of v6, /device:TPU:1, one launch (start us, length us, event | category | flops | bytes accessed | tf_op | source)
XLA Modules:
  0.0 94.3 jit_solution(6539676320226269816)
XLA Ops:
  0.0 93.1 %shard_map.37 = bf16[512,1536]{1,0:T(8,128)(2,1)S(1)} custom-call(bf16[512,384]{1,0:T(8,128)(2,1)} %t_ref.1, bf16[1536,768]{1,0:T(8,128)(2,1)} %w_ref.1, f32[12,128]{1,0:T(8,128)} %bitcast.1), custom_call_target="tpu_custom_call" | custom-call | tf_op jit(solution)/shard_map/pallas_call | solution.py:343
  93.2 1.1 %copy.5 = bf16[512,1536]{1,0:T(8,128)(2,1)} copy(bf16[512,1536]{1,0:T(8,128)(2,1)S(1)} %shard_map.37) | data formatting | bytes 3145728
